TPU v7x, 32 devices: a whole 2x2x4 slice. The times are simulated.
32 devices in a mesh: head: 8 (over z, y), ctx: 4 (over x, core).
Axes of the slice: x: 2, y: 2, z: 4, core: 2. Of those that a mesh axis runs over, the one named last changes fastest.
Arguments:
- query: bfloat16 [3072, 4096], P(('ctx', 'head')), may hold values from -8 to 8
- key: bfloat16 [3072, 2048], P(('ctx', 'head')), may hold values from -8 to 8
- value: bfloat16 [3072, 2048], P(('ctx', 'head')), may hold values from -8 to 8
- block_order: int32 [8], replicated, may hold values from 0 to 7, each once
Outputs:
- attended: bfloat16 [3072, 4096], P('ctx', 'head')
Inputs may be any that keep to these rules, and one draw needn't show every extreme that they name: `block_order`: each storage block index 0 to 7 appears exactly once.
All inputs are finite; a program needn't handle non-finite values.
Results may differ from a plain program's by a relative error of at most 0.0049.
Values may be sent and summed in bfloat16 or wider, within the bound.
A program may use at most 128 MiB of HBM per device.

v0:
```python
import jax
import jax.numpy as jnp
from jax import lax
from jax.sharding import PartitionSpec as P

HEAD_WIDTH = 128
query_scale = 1.0 / 12.0
softcap_limit = 50.0


def from_behind(value, axis, by):
    size = lax.axis_size(axis)
    return lax.ppermute(value, axis, [(i, (i + by) % size) for i in range(size)])


def block_pos(block_order, which_block, block_len):
    first = lax.dynamic_index_in_dim(block_order, which_block, 0, keepdims=False)
    return first * block_len + lax.iota(jnp.int32, block_len)


def add_block(totals, query_rows, query_pos, key_block, value_block, key_pos):
    numerator, denominator = totals
    scores = (
        jnp.einsum("rhgd,khd->hgrk", query_rows, key_block, preferred_element_type=jnp.float32)
        * query_scale
    )
    capped = softcap_limit * jnp.tanh(scores / softcap_limit)
    visible = key_pos[None, :] <= query_pos[:, None]
    weights = jnp.where(visible[None, None], jnp.exp(capped), jnp.zeros_like(capped))
    denominator = denominator + jnp.sum(weights, axis=-1)
    numerator = numerator + jnp.einsum(
        "hgrk,khd->rhgd",
        weights.astype(jnp.bfloat16),
        value_block,
        preferred_element_type=jnp.float32,
    )
    return (numerator, denominator)


def shards(query, key, value, block_order):
    query, key, value = (
        lax.all_to_all(query, "head", split_axis=1, concat_axis=0, tiled=True),
        lax.all_to_all(key, "head", split_axis=1, concat_axis=0, tiled=True),
        lax.all_to_all(value, "head", split_axis=1, concat_axis=0, tiled=True),
    )
    row_count = query.shape[0]
    block_len = row_count // 2
    kv_heads = key.shape[1] // HEAD_WIDTH
    group_size = query.shape[1] // key.shape[1]
    query_rows = query.reshape(row_count, kv_heads, group_size, HEAD_WIDTH)
    kv_pair = jnp.stack(
        [
            key.reshape(row_count, kv_heads, HEAD_WIDTH),
            value.reshape(row_count, kv_heads, HEAD_WIDTH),
        ]
    )
    cycle_size = lax.axis_size("ctx")
    cycle_index = lax.axis_index("ctx")
    query_pos = jnp.concatenate(
        [
            block_pos(block_order, 2 * cycle_index, block_len),
            block_pos(block_order, 2 * cycle_index + 1, block_len),
        ]
    )
    start_totals = (
        jnp.zeros((row_count, kv_heads, group_size, HEAD_WIDTH), jnp.float32),
        jnp.zeros((kv_heads, group_size, row_count), jnp.float32),
    )

    def add_shard(totals, held, source):
        for which_half in range(2):
            lower = which_half * block_len
            key_pos = block_pos(block_order, 2 * source + which_half, block_len)
            totals = add_block(
                totals,
                query_rows,
                query_pos,
                held[0, lower : lower + block_len],
                held[1, lower : lower + block_len],
                key_pos,
            )
        return totals

    totals = add_shard(start_totals, kv_pair, cycle_index)

    def from_lower(held):
        return from_behind(held, "ctx", 1)

    def turn_both(turn_index, state):
        forward_kv, backward_kv, sums = state
        forward_kv = from_lower(forward_kv)
        backward_kv = from_behind(backward_kv, "ctx", -1)
        sums = add_shard(sums, forward_kv, (cycle_index - turn_index) % cycle_size)
        sums = add_shard(sums, backward_kv, (cycle_index + turn_index) % cycle_size)
        return (forward_kv, backward_kv, sums)

    forward_kv, backward_kv, totals = lax.fori_loop(
        1, cycle_size // 2, turn_both, (kv_pair, kv_pair, totals)
    )
    forward_kv = from_lower(forward_kv)
    totals = add_shard(totals, forward_kv, (cycle_index + cycle_size // 2) % cycle_size)
    numerator, denominator = totals
    result = numerator / jnp.transpose(denominator, (2, 0, 1))[..., None]
    return result.reshape(row_count, kv_heads * group_size * HEAD_WIDTH).astype(jnp.bfloat16)


def solution(mesh):
    placed = (P(("ctx", "head"), None), P(("ctx", "head"), None), P(("ctx", "head"), None), P())
    return jax.shard_map(
        shards, mesh=mesh, in_specs=placed, out_specs=P("ctx", "head"), check_vma=False
    )
```

profile of v0, /device:TPU:1, one launch (start us, length us, event | category | flops | bytes accessed | tf_op | source)
XLA Modules:
  0.0 99.2 jit_solution(4919566508490505928)
XLA Ops:
  0.0 1.8 %copy.134 = bf16[12,8,8,256]{3,2,0,1:T(8,128)(2,1)} copy(bf16[12,8,8,256]{3,2,1,0:T(8,128)(2,1)} %bitcast.235) | data formatting | bytes 786432 | tf_op jit(solution)/shard_map/all_to_all | solution.py:43
  1.8 6.4 %all-to-all-start = ((bf16[96,8,256]{2,0,1:T(8,128)(2,1)}), bf16[96,8,256]{2,0,1:T(8,128)(2,1)S(1)}, u32[]{:S(2)}, u32[]{:S(2)}) async-start(bf16[96,8,256]{2,0,1:T(8,128)(2,1)} %bitcast.228), calls=%async_computation | async-start | bytes 786432 | tf_op jit(solution)/shard_map/all_to_all | solution.py:43
  8.1 1.8 %copy.135 = bf16[12,8,8,256]{3,2,0,1:T(8,128)(2,1)} copy(bf16[12,8,8,256]{3,2,1,0:T(8,128)(2,1)} %bitcast.236) | data formatting | bytes 786432 | tf_op jit(solution)/shard_map/all_to_all | solution.py:44
  9.9 7.4 %all-to-all-done = bf16[96,8,256]{2,0,1:T(8,128)(2,1)S(1)} async-done(((bf16[96,8,256]{2,0,1:T(8,128)(2,1)}), bf16[96,8,256]{2,0,1:T(8,128)(2,1)S(1)}, u32[]{:S(2)}, u32[]{:S(2)}) %all-to-all-start) | async-done | bytes 393248 | tf_op jit(solution)/shard_map/all_to_all | solution.py:43
  17.3 6.1 %all-to-all-start.2 = ((bf16[96,8,256]{2,0,1:T(8,128)(2,1)}), bf16[96,8,256]{2,0,1:T(8,128)(2,1)S(1)}, u32[]{:S(2)}, u32[]{:S(2)}) async-start(bf16[96,8,256]{2,0,1:T(8,128)(2,1)} %bitcast.229), calls=%async_computation.2 | async-start | bytes 786432 | tf_op jit(solution)/shard_map/all_to_all | solution.py:44
  23.4 1.6 %fusion.88 = (s32[1]{0:T(128)}, s32[1]{0:T(128)}, s32[1]{0:T(128)}, s32[1]{0:T(128)}, s32[1]{0:T(128)}, /*index=5*/s32[1]{0:T(128)}, s32[1]{0:T(128)}, s32[1]{0:T(128)}) fusion(s32[8]{0:T(128)} %param.7, s32[]{:T(128)S(6)} %select_n.95, s32[]{:T(128)S(6)} %select_n.90, s32[]{:T(128)S(6)} %select_n.88, s32[]{:T(128)S(6)} %select_n.85, s32[]{:T(128)S(6)} %select_n.83, ...), kind=kLoop, calls=%fused_computation.129 | loop fusion | bytes 96 | tf_op jit(solution)/shard_map/jit(dynamic_index_in_dim)/dynamic_slice | solution.py:17
  28.8 2.1 %copy.133 = bf16[12,8,8,512]{3,2,0,1:T(8,128)(2,1)} copy(bf16[12,8,8,512]{3,2,1,0:T(8,128)(2,1)} %bitcast.234) | data formatting | bytes 1572864 | tf_op jit(solution)/shard_map/all_to_all | solution.py:42
  30.9 1.6 %all-to-all-done.2 = bf16[96,8,256]{2,0,1:T(8,128)(2,1)S(1)} async-done(((bf16[96,8,256]{2,0,1:T(8,128)(2,1)}), bf16[96,8,256]{2,0,1:T(8,128)(2,1)S(1)}, u32[]{:S(2)}, u32[]{:S(2)}) %all-to-all-start.2) | async-done | bytes 393248 | tf_op jit(solution)/shard_map/all_to_all | solution.py:44
  32.5 6.1 %all-to-all-start.1 = ((bf16[96,8,512]{2,0,1:T(8,128)(2,1)}), bf16[96,8,512]{2,0,1:T(8,128)(2,1)S(1)}, u32[]{:S(2)}, u32[]{:S(2)}) async-start(bf16[96,8,512]{2,0,1:T(8,128)(2,1)} %bitcast.227), calls=%async_computation.1 | async-start | bytes 1572864 | tf_op jit(solution)/shard_map/all_to_all | solution.py:42
  39.8 2.4 %broadcast_compare_fusion = (pred[768,384]{0,1:T(8,128)(4,1)S(1)}, pred[768,384]{0,1:T(8,128)(4,1)}, pred[768,384]{0,1:T(8,128)(4,1)S(1)}, pred[768,384]{0,1:T(8...) fusion(s32[768]{0:T(1024)S(1)} %pad_add_fusion, ...), kind=kLoop, calls=%fused_computation.49 | loop fusion | flops 2359296 | bytes 2374656 | tf_op jit(solution)/shard_map/le | solution.py:28
  42.4 0.9 fusion.87
  43.2 0.8 copy_dynamic-update-slice_fusion
  44.0 2.2 %collective-permute-start = (bf16[2,768,2,128]{3,1,2,0:T(8,128)(2,1)}, bf16[2,768,2,128]{3,1,2,0:T(8,128)(2,1)}, u32[]{:S(2)}, u32[]{:S(2)}) collective-permute-start(bf16[2,768,2,128]{3,1,2,0:T(8,128)(2,1)} %copy_dynamic-update-slice_fusion), channel_id=1, source_target_pairs={{0,1},{1,2},{2,3},{3,0},{4,5},{5,6},{6,7},{7,4},{8,9},{9,10},{10,1... | collective-permute-start | bytes 2359304 | tf_op jit(solution)/shard_map/while/body/eval_jaxpr/ppermute | solution.py:13
  46.9 10.7 %all-to-all-done.1 = bf16[96,8,512]{2,0,1:T(8,128)(2,1)S(1)} async-done(((bf16[96,8,512]{2,0,1:T(8,128)(2,1)}), bf16[96,8,512]{2,0,1:T(8,128)(2,1)S(1)}, u32[]{:S(2)}, u32[]{:S(2)}) %all-to-all-start.1) | async-done | bytes 786464 | tf_op jit(solution)/shard_map/all_to_all | solution.py:42
  57.8 2.8 %fusion = (f32[2,2,768]{2,1,0:T(2,128)S(1)}, f32[2,384,768,2]{2,1,3,0:T(8,128)S(1)}) fusion(pred[768,384]{0,1:T(8,128)(4,1)} %get-tuple-element.46, bf16[768,2,2,128]{3,2,1,0:T(2,128)(2,1)S(1)} %reshape.260, bf16[1,768,2,128]{3,1,2,0:T(8,128)(2,1)S(1)} %get-tuple-element.25), kind=kOutput, calls=%fused_computation.8 | convolution fusion | flops 306705408 | bytes 6008832 | tf_op jit(solution)/shard_map/rhgd,khd->hgrk/dot_general | solution.py:24
  60.6 1.8 %fusion.30 = f32[2,2,768,128]{2,3,1,0:T(8,128)S(1)} fusion(f32[2,384,768,2]{2,1,3,0:T(8,128)S(1)} %get-tuple-element.68, pred[768,384]{0,1:T(8,128)(4,1)S(1)} %copy-done.3, bf16[1,384,2,128]{1,3,2,0:T(8,128)(2,1)S(1)} %copy.90), kind=kOutput, calls=%fused_computation.31 | convolution fusion | flops 306708480 | bytes 6782976 | tf_op jit(solution)/shard_map/hgrk,khd->rhgd/dot_general | solution.py:31
  62.4 1.8 %fusion.2 = (f32[2,2,768]{2,1,0:T(2,128)S(1)}, f32[2,384,768,2]{2,1,3,0:T(8,128)S(1)}) fusion(pred[768,384]{0,1:T(8,128)(4,1)S(1)} %copy-done.2, bf16[768,2,2,128]{3,2,1,0:T(2,128)(2,1)S(1)} %reshape.260, bf16[1,768,2,128]{3,1,2,0:T(8,128)(2,1)S(1)} %get-tuple-element.25), kind=kOutput, calls=%fused_computation.10 | convolution fusion | flops 306705408 | bytes 6008832 | tf_op jit(solution)/shard_map/rhgd,khd->hgrk/dot_general | solution.py:24
  64.2 1.8 %fusion.28 = f32[2,2,768,128]{2,3,1,0:T(8,128)S(1)} fusion(f32[2,384,768,2]{2,1,3,0:T(8,128)S(1)} %get-tuple-element.70, pred[768,384]{0,1:T(8,128)(4,1)S(1)} %copy-done.2, bf16[1,384,2,128]{1,3,2,0:T(8,128)(2,1)S(1)} %copy.91), kind=kOutput, calls=%fused_computation.30 | convolution fusion | flops 306708480 | bytes 6782976 | tf_op jit(solution)/shard_map/hgrk,khd->rhgd/dot_general | solution.py:31
  66.0 3.5 %collective-permute-start.2 = (bf16[2,768,2,128]{3,1,2,0:T(8,128)(2,1)}, bf16[2,768,2,128]{3,1,2,0:T(8,128)(2,1)S(1)}, u32[]{:S(2)}, u32[]{:S(2)}) collective-permute-start(bf16[2,768,2,128]{3,1,2,0:T(8,128)(2,1)} %collective-permute-done), channel_id=1, source_target_pairs={{0,1},{1,2},{2,3},{3,0},{4,5},{5,6},{6,7},{7,4},{8,9},{9,10},{10,1... | collective-permute-start | bytes 2359304 | tf_op jit(solution)/shard_map/ppermute | solution.py:13
  69.5 2.7 %fusion.10 = (f32[2,2,768]{2,1,0:T(2,128)S(1)}, f32[2,384,768,2]{2,1,3,0:T(8,128)S(1)}) fusion(pred[768,384]{0,1:T(8,128)(4,1)S(1)} %copy-done.1, bf16[768,2,2,128]{3,2,1,0:T(2,128)(2,1)S(1)} %reshape.260, bf16[2,768,2,128]{3,1,2,0:T(8,128)(2,1)} %collective-permute-done.1), kind=kOutput, calls=%fused_computation.18 | convolution fusion | flops 306705408 | bytes 6008832 | tf_op jit(solution)/shard_map/while/body/eval_jaxpr/rhgd,khd->hgrk/dot_general | solution.py:24
  72.2 2.6 %fusion.20 = f32[2,128,2,768]{3,1,2,0:T(8,128)S(1)} fusion(f32[2,384,768,2]{2,1,3,0:T(8,128)S(1)} %get-tuple-element.60, pred[768,384]{0,1:T(8,128)(4,1)S(1)} %copy-done.1, bf16[2,768,2,128]{3,1,2,0:T(8,128)(2,1)} %collective-permute-done.1), kind=kOutput, calls=%fused_computation.26 | convolution fusion | flops 306708480 | bytes 6782976 | tf_op jit(solution)/shard_map/while/body/eval_jaxpr/hgrk,khd->rhgd/dot_general | solution.py:31
  74.8 2.7 %fusion.8 = (f32[2,2,768]{2,1,0:T(2,128)S(1)}, f32[2,384,768,2]{2,1,3,0:T(8,128)S(1)}) fusion(pred[768,384]{0,1:T(8,128)(4,1)S(1)} %copy-done, bf16[768,2,2,128]{3,2,1,0:T(2,128)(2,1)S(1)} %reshape.260, bf16[2,768,2,128]{3,1,2,0:T(8,128)(2,1)} %collective-permute-done.1), kind=kOutput, calls=%fused_computation.16 | convolution fusion | flops 306705408 | bytes 6008832 | tf_op jit(solution)/shard_map/while/body/eval_jaxpr/rhgd,khd->hgrk/dot_general | solution.py:24
  77.5 2.5 %fusion.22 = f32[2,128,2,768]{3,1,2,0:T(8,128)S(1)} fusion(f32[2,384,768,2]{2,1,3,0:T(8,128)S(1)} %get-tuple-element.62, pred[768,384]{0,1:T(8,128)(4,1)S(1)} %copy-done, bf16[2,768,2,128]{3,1,2,0:T(8,128)(2,1)} %collective-permute-done.1), kind=kOutput, calls=%fused_computation.27 | convolution fusion | flops 306708480 | bytes 6782976 | tf_op jit(solution)/shard_map/while/body/eval_jaxpr/hgrk,khd->rhgd/dot_general | solution.py:31
  80.1 2.7 %fusion.6 = (f32[2,2,768]{2,1,0:T(2,128)S(1)}, f32[2,384,768,2]{2,1,3,0:T(8,128)S(1)}) fusion(pred[768,384]{0,1:T(8,128)(4,1)S(1)} %get-tuple-element.40, bf16[768,2,2,128]{3,2,1,0:T(2,128)(2,1)S(1)} %reshape.260, bf16[2,768,2,128]{3,1,2,0:T(8,128)(2,1)} %collective-permute-done), kind=kOutput, calls=%fused_computation.14 | convolution fusion | flops 306705408 | bytes 6008832 | tf_op jit(solution)/shard_map/while/body/eval_jaxpr/rhgd,khd->hgrk/dot_general | solution.py:24
  82.8 2.5 %fusion.24 = f32[2,128,2,768]{3,1,2,0:T(8,128)S(1)} fusion(f32[2,384,768,2]{2,1,3,0:T(8,128)S(1)} %get-tuple-element.64, pred[768,384]{0,1:T(8,128)(4,1)S(1)} %get-tuple-element.40, bf16[2,768,2,128]{3,1,2,0:T(8,128)(2,1)} %collective-permute-done), kind=kOutput, calls=%fused_computation.28 | convolution fusion | flops 306708480 | bytes 6782976 | tf_op jit(solution)/shard_map/while/body/eval_jaxpr/hgrk,khd->rhgd/dot_general | solution.py:31
  85.3 2.7 %fusion.4 = (f32[2,2,768]{2,1,0:T(2,128)S(1)}, f32[2,384,768,2]{2,1,3,0:T(8,128)S(1)}) fusion(pred[768,384]{0,1:T(8,128)(4,1)S(1)} %get-tuple-element.29, bf16[768,2,2,128]{3,2,1,0:T(2,128)(2,1)S(1)} %reshape.260, bf16[2,768,2,128]{3,1,2,0:T(8,128)(2,1)} %collective-permute-done), kind=kOutput, calls=%fused_computation.12 | convolution fusion | flops 306705408 | bytes 6008832 | tf_op jit(solution)/shard_map/while/body/eval_jaxpr/rhgd,khd->hgrk/dot_general | solution.py:24
  88.1 2.7 %fusion.26 = f32[2,128,2,768]{3,1,2,0:T(8,128)S(1)} fusion(f32[2,384,768,2]{2,1,3,0:T(8,128)S(1)} %get-tuple-element.66, pred[768,384]{0,1:T(8,128)(4,1)S(1)} %get-tuple-element.29, bf16[2,768,2,128]{3,1,2,0:T(8,128)(2,1)} %collective-permute-done), kind=kOutput, calls=%fused_computation.29 | convolution fusion | flops 306708480 | bytes 6782976 | tf_op jit(solution)/shard_map/while/body/eval_jaxpr/hgrk,khd->rhgd/dot_general | solution.py:31
  90.8 1.8 %fusion.12 = (f32[2,2,768]{2,1,0:T(2,128)S(1)}, f32[2,384,768,2]{2,1,3,0:T(8,128)S(1)}) fusion(pred[768,384]{0,1:T(8,128)(4,1)S(1)} %get-tuple-element.45, bf16[768,2,2,128]{3,2,1,0:T(2,128)(2,1)S(1)} %reshape.260, bf16[2,768,2,128]{3,1,2,0:T(8,128)(2,1)S(1)} %collective-permute-done.2), kind=kOutput, calls=%fused_computation.20 | convolution fusion | flops 306705408 | bytes 6008832 | tf_op jit(solution)/shard_map/rhgd,khd->hgrk/dot_general | solution.py:24
  92.6 1.8 %fusion.14 = (f32[2,2,768]{2,1,0:T(2,128)S(1)}, f32[2,384,768,2]{2,1,3,0:T(8,128)S(1)}) fusion(pred[768,384]{0,1:T(8,128)(4,1)S(1)} %get-tuple-element.27, bf16[768,2,2,128]{3,2,1,0:T(2,128)(2,1)S(1)} %reshape.260, bf16[2,768,2,128]{3,1,2,0:T(8,128)(2,1)S(1)} %collective-permute-done.2), kind=kOutput, calls=%fused_computation.22 | convolution fusion | flops 306705408 | bytes 6008832 | tf_op jit(solution)/shard_map/rhgd,khd->hgrk/dot_general | solution.py:24
  94.4 1.6 %fusion.18 = f32[2,128,2,768]{3,1,2,0:T(8,128)S(1)} fusion(f32[2,384,768,2]{2,1,3,0:T(8,128)S(1)} %get-tuple-element.58, pred[768,384]{0,1:T(8,128)(4,1)S(1)} %get-tuple-element.45, bf16[2,768,2,128]{3,1,2,0:T(8,128)(2,1)S(1)} %collective-permute-done.2), kind=kOutput, calls=%fused_computation.25 | convolution fusion | flops 306708480 | bytes 6782976 | tf_op jit(solution)/shard_map/hgrk,khd->rhgd/dot_general | solution.py:31
  96.1 2.0 %fusion.41 = bf16[768,2,2,128]{0,3,2,1:T(8,128)(2,1)S(1)} fusion(f32[2,128,2,768]{3,1,2,0:T(8,128)S(1)} %fusion.18, f32[2,128,2,768]{3,1,2,0:T(8,128)S(1)} %fusion.20, f32[2,128,2,768]{3,1,2,0:T(8,128)S(1)} %fusion.22, f32[2,128,2,768]{3,1,2,0:T(8,128)S(1)} %fusion.24, f32[2,128,2,768]{3,1,2,0:T(8,128)S(1)} %fusion.26, f32[2,2,768,128]{2,3,1,0:T(8,128)S(1)} %fusion.30, ...), kind=kOutput, calls=%fused_computation.42 | convolution fusion | flops 310247424 | bytes 17018880 | tf_op jit(solution)/shard_map/hgrk,khd->rhgd/dot_general | solution.py:31
  98.1 1.2 %copy.53 = bf16[768,512]{1,0:T(8,128)(2,1)} copy(bf16[768,512]{0,1:T(8,128)(2,1)S(1)} %bitcast.230) | data formatting | bytes 1572864 | tf_op jit(solution)/shard_map/convert_element_type | solution.py:104
  (24 shorter events, 1.1 us)
Async XLA Ops:
  1.8 15.5 %all-to-all-start = ((bf16[96,8,256]{2,0,1:T(8,128)(2,1)}), bf16[96,8,256]{2,0,1:T(8,128)(2,1)S(1)}, u32[]{:S(2)}, u32[]{:S(2)}) async-start(bf16[96,8,256]{2,0,1:T(8,128)(2,1)} %bitcast.228), calls=%async_computation | async-start | bytes 786432 | tf_op jit(solution)/shard_map/all_to_all | solution.py:43
  17.3 15.2 %all-to-all-start.2 = ((bf16[96,8,256]{2,0,1:T(8,128)(2,1)}), bf16[96,8,256]{2,0,1:T(8,128)(2,1)S(1)}, u32[]{:S(2)}, u32[]{:S(2)}) async-start(bf16[96,8,256]{2,0,1:T(8,128)(2,1)} %bitcast.229), calls=%async_computation.2 | async-start | bytes 786432 | tf_op jit(solution)/shard_map/all_to_all | solution.py:44
  32.5 25.1 %all-to-all-start.1 = ((bf16[96,8,512]{2,0,1:T(8,128)(2,1)}), bf16[96,8,512]{2,0,1:T(8,128)(2,1)S(1)}, u32[]{:S(2)}, u32[]{:S(2)}) async-start(bf16[96,8,512]{2,0,1:T(8,128)(2,1)} %bitcast.227), calls=%async_computation.1 | async-start | bytes 1572864 | tf_op jit(solution)/shard_map/all_to_all | solution.py:42
  44.0 22.0 %collective-permute-start = (bf16[2,768,2,128]{3,1,2,0:T(8,128)(2,1)}, bf16[2,768,2,128]{3,1,2,0:T(8,128)(2,1)}, u32[]{:S(2)}, u32[]{:S(2)}) collective-permute-start(bf16[2,768,2,128]{3,1,2,0:T(8,128)(2,1)} %copy_dynamic-update-slice_fusion), channel_id=1, source_target_pairs={{0,1},{1,2},{2,3},{3,0},{4,5},{5,6},{6,7},{7,4},{8,9},{9,10},{10,1... | collective-permute-start | bytes 2359304 | tf_op jit(solution)/shard_map/while/body/eval_jaxpr/ppermute | solution.py:13
  46.3 23.2 %collective-permute-start.1 = (bf16[2,768,2,128]{3,1,2,0:T(8,128)(2,1)}, bf16[2,768,2,128]{3,1,2,0:T(8,128)(2,1)}, u32[]{:S(2)}, u32[]{:S(2)}) collective-permute-start(bf16[2,768,2,128]{3,1,2,0:T(8,128)(2,1)} %copy_dynamic-update-slice_fusion), channel_id=1, source_target_pairs={{0,3},{1,0},{2,1},{3,2},{4,7},{5,4},{6,5},{7,6},{8,11},{9,8},{10,9... | collective-permute-start | bytes 2359304 | tf_op jit(solution)/shard_map/while/body/eval_jaxpr/ppermute | solution.py:13
  57.8 2.8 %copy-start.3 = (pred[768,384]{0,1:T(8,128)(4,1)S(1)}, pred[768,384]{0,1:T(8,128)(4,1)}, u32[]{:S(2)}) copy-start(pred[768,384]{0,1:T(8,128)(4,1)} %get-tuple-element.46) | copy-start | bytes 884740
  60.6 1.8 %copy-start.2 = (pred[768,384]{0,1:T(8,128)(4,1)S(1)}, pred[768,384]{0,1:T(8,128)(4,1)}, u32[]{:S(2)}) copy-start(pred[768,384]{0,1:T(8,128)(4,1)} %get-tuple-element.28) | copy-start | bytes 884740
  64.2 5.3 %copy-start.1 = (pred[768,384]{0,1:T(8,128)(4,1)S(1)}, pred[768,384]{0,1:T(8,128)(4,1)}, u32[]{:S(2)}) copy-start(pred[768,384]{0,1:T(8,128)(4,1)} %get-tuple-element.44) | copy-start | bytes 884740
  66.0 24.8 %collective-permute-start.2 = (bf16[2,768,2,128]{3,1,2,0:T(8,128)(2,1)}, bf16[2,768,2,128]{3,1,2,0:T(8,128)(2,1)S(1)}, u32[]{:S(2)}, u32[]{:S(2)}) collective-permute-start(bf16[2,768,2,128]{3,1,2,0:T(8,128)(2,1)} %collective-permute-done), channel_id=1, source_target_pairs={{0,1},{1,2},{2,3},{3,0},{4,5},{5,6},{6,7},{7,4},{8,9},{9,10},{10,1... | collective-permute-start | bytes 2359304 | tf_op jit(solution)/shard_map/ppermute | solution.py:13
  72.2 2.6 %copy-start = (pred[768,384]{0,1:T(8,128)(4,1)S(1)}, pred[768,384]{0,1:T(8,128)(4,1)}, u32[]{:S(2)}) copy-start(pred[768,384]{0,1:T(8,128)(4,1)} %get-tuple-element.42) | copy-start | bytes 884740
where the time goes:
time: 100 us; the launch traced here: 99.2 us
  matrix products  36.6 us (37%)
  starting transfers between devices  24.2 us (24%)
  waiting for transfers between devices  19.7 us (20%)
  local copies, waits for them, and re-layouts  11.1 us (11%)
  between operations  5.27 us (5%)
  other arithmetic  2.43 us (2%)
    dot_general x8, matrix products, add_block(): jnp.einsum('rhgd,khd->hgrk', query_rows, key_block, preferred_element_typ...  19 us
    dot_general x8, matrix products, add_block(): jnp.einsum('hgrk,khd->rhgd', weights.astype(jnp.bfloat16), value_block, p...  17.6 us
    all_to_all x1, waiting for transfers between devices, shards(): lax.all_to_all(query, 'head', split_axis=1, concat_axis=0, tiled=True)  10.7 us
    all_to_all x1, waiting for transfers between devices, shards(): lax.all_to_all(key, 'head', split_axis=1, concat_axis=0, tiled=True)  7.41 us
    all_to_all x1, starting transfers between devices, shards(): lax.all_to_all(key, 'head', split_axis=1, concat_axis=0, tiled=True)  6.37 us
    all_to_all x1, starting transfers between devices, shards(): lax.all_to_all(query, 'head', split_axis=1, concat_axis=0, tiled=True)  6.06 us
    all_to_all x1, starting transfers between devices, shards(): lax.all_to_all(value, 'head', split_axis=1, concat_axis=0, tiled=True)  6.06 us
    ppermute x3, starting transfers between devices, from_behind(): lax.ppermute(value, axis, [(i, (i + by) % size) for i in range(size)])  5.67 us
  transfers between devices with their start and end apart: 6, of which 3 were waited for; matrix products, arithmetic and copies ran while one was open for 40% of the time, Pallas kernels for 0%

commit v1 on v0

--- a/solution.py
+++ b/solution.py
@@ -38,9 +38,18 @@
 
 
 def shards(query, key, value, block_order):
+    keep_up_seats_all = lambda s0, net_axis: jnp.concatenate(
+        lax.all_to_all(
+            jnp.stack(jnp.split(s0, lax.axis_size(net_axis), axis=1), axis=0),
+            axis_name=net_axis,
+            split_axis=0,
+            concat_axis=0,
+        ),
+        axis=0,
+    )
     query, key, value = (
         lax.all_to_all(query, "head", split_axis=1, concat_axis=0, tiled=True),
-        lax.all_to_all(key, "head", split_axis=1, concat_axis=0, tiled=True),
+        keep_up_seats_all(key, "head"),
         lax.all_to_all(value, "head", split_axis=1, concat_axis=0, tiled=True),
     )
     row_count = query.shape[0]

time: 100 us -> 110 us (1.10)
  local copies, waits for them, and re-layouts: 11.1 us -> 20.7 us
    unnamed x10 -> x17, local copies, waits for them, and re-layouts: 0.37 us -> 10.3 us
    all_to_all x1 -> x0, local copies, waits for them, and re-layouts: 1.77 us -> none  [shards(): lax.all_to_all(key, 'head', split_axis=1, concat_axis=0, tiled=True)]
    another operation x0 -> x1, local copies, waits for them, and re-layouts: none -> 1.42 us  [shards(): jnp.stack(jnp.split(s0, lax.axis_size(net_axis), axis=1), axis=0)]
  transfers between devices with their start and end apart: 6 -> 6, of which waited for: 3 -> 3; matrix products, arithmetic and copies ran while one was open for 40% -> 37% of each run, Pallas kernels for 0% -> 0%
where the time goes in v1:
time: 110 us; the launch traced here: 109 us
  matrix products  36.6 us (33%)
  starting transfers between devices  24.2 us (22%)
  local copies, waits for them, and re-layouts  20.7 us (19%)
  waiting for transfers between devices  19.7 us (18%)
  between operations  5.27 us (5%)
  other arithmetic  2.43 us (2%)
    dot_general x8, matrix products, add_block(): jnp.einsum('rhgd,khd->hgrk', query_rows, key_block, preferred_element_typ...  19 us
    dot_general x8, matrix products, add_block(): jnp.einsum('hgrk,khd->rhgd', weights.astype(jnp.bfloat16), value_block, p...  17.6 us
    all_to_all x1, waiting for transfers between devices, shards(): lax.all_to_all(query, 'head', split_axis=1, concat_axis=0, tiled=True)  10.7 us
    unnamed x17, local copies, waits for them, and re-layouts  10.3 us
    all_to_all x1, waiting for transfers between devices, shards(): lax.all_to_all(jnp.stack(jnp.split(s0, lax.axis_size(net_axis), axis=1),...  7.41 us
    all_to_all x1, starting transfers between devices, shards(): lax.all_to_all(jnp.stack(jnp.split(s0, lax.axis_size(net_axis), axis=1),...  6.37 us
    all_to_all x1, starting transfers between devices, shards(): lax.all_to_all(query, 'head', split_axis=1, concat_axis=0, tiled=True)  6.06 us
    all_to_all x1, starting transfers between devices, shards(): lax.all_to_all(value, 'head', split_axis=1, concat_axis=0, tiled=True)  6.06 us
  transfers between devices with their start and end apart: 6, of which 3 were waited for; matrix products, arithmetic and copies ran while one was open for 37% of the time, Pallas kernels for 0%

profile of v1, /device:TPU:1, one launch (start us, length us, event | category | flops | bytes accessed | tf_op | source)
XLA Modules:
  0.0 108.8 jit_solution(4893535403671913944)
XLA Ops:
  0.0 1.4 %bitcast_dynamic-update-slice_fusion.7 = bf16[8,96,256]{2,1,0:T(8,128)(2,1)} fusion(bf16[96,2048]{1,0:T(8,128)(2,1)} %param.5), kind=kLoop, calls=%fused_computation.98 | loop fusion | bytes 98304
  1.4 1.4 %bitcast_dynamic-update-slice_fusion.6 = bf16[8,96,256]{2,1,0:T(8,128)(2,1)} fusion(bf16[8,96,256]{2,1,0:T(8,128)(2,1)} %bitcast_dynamic-update-slice_fusion.7, bf16[96,2048]{1,0:T(8,128)(2,1)} %param.5), kind=kLoop, calls=%fused_computation.97 | loop fusion | bytes 98304
  5.7 1.4 %bitcast_dynamic-update-slice_fusion.3 = bf16[8,96,256]{2,1,0:T(8,128)(2,1)} fusion(bf16[8,96,256]{2,1,0:T(8,128)(2,1)} %bitcast_dynamic-update-slice_fusion.4, bf16[96,2048]{1,0:T(8,128)(2,1)} %param.5), kind=kLoop, calls=%fused_computation.94 | loop fusion | bytes 98304
  9.9 1.4 %bitcast_dynamic-update-slice_fusion = bf16[8,96,256]{2,1,0:T(8,128)(2,1)} fusion(bf16[8,96,256]{2,1,0:T(8,128)(2,1)} %bitcast_dynamic-update-slice_fusion.1, bf16[96,2048]{1,0:T(8,128)(2,1)} %param.5), kind=kLoop, calls=%fused_computation.91 | loop fusion | bytes 98304 | tf_op jit(solution)/shard_map/stack | solution.py:43
  11.4 6.4 %all-to-all-start = ((bf16[8,96,256]{2,1,0:T(8,128)(2,1)}), bf16[8,96,256]{2,1,0:T(8,128)(2,1)S(1)}, u32[]{:S(2)}, u32[]{:S(2)}) async-start(bf16[8,96,256]{2,1,0:T(8,128)(2,1)} %bitcast_dynamic-update-slice_fusion), calls=%async_computation | async-start | bytes 786432 | tf_op jit(solution)/shard_map/all_to_all | solution.py:42
  17.7 1.8 %copy.131 = bf16[12,8,8,256]{3,2,0,1:T(8,128)(2,1)} copy(bf16[12,8,8,256]{3,2,1,0:T(8,128)(2,1)} %bitcast.245) | data formatting | bytes 786432 | tf_op jit(solution)/shard_map/all_to_all | solution.py:53
  19.5 7.4 %all-to-all-done = bf16[8,96,256]{2,1,0:T(8,128)(2,1)S(1)} async-done(((bf16[8,96,256]{2,1,0:T(8,128)(2,1)}), bf16[8,96,256]{2,1,0:T(8,128)(2,1)S(1)}, u32[]{:S(2)}, u32[]{:S(2)}) %all-to-all-start) | async-done | bytes 393248 | tf_op jit(solution)/shard_map/all_to_all | solution.py:42
  26.9 6.1 %all-to-all-start.2 = ((bf16[96,8,256]{2,0,1:T(8,128)(2,1)}), bf16[96,8,256]{2,0,1:T(8,128)(2,1)S(1)}, u32[]{:S(2)}, u32[]{:S(2)}) async-start(bf16[96,8,256]{2,0,1:T(8,128)(2,1)} %bitcast.240), calls=%async_computation.2 | async-start | bytes 786432 | tf_op jit(solution)/shard_map/all_to_all | solution.py:53
  33.0 1.6 %fusion.88 = (s32[1]{0:T(128)}, s32[1]{0:T(128)}, s32[1]{0:T(128)}, s32[1]{0:T(128)}, s32[1]{0:T(128)}, /*index=5*/s32[1]{0:T(128)}, s32[1]{0:T(128)}, s32[1]{0:T(128)}) fusion(s32[8]{0:T(128)} %param.7, s32[]{:T(128)S(6)} %select_n.95, s32[]{:T(128)S(6)} %select_n.90, s32[]{:T(128)S(6)} %select_n.88, s32[]{:T(128)S(6)} %select_n.85, s32[]{:T(128)S(6)} %select_n.83, ...), kind=kLoop, calls=%fused_computation.136 | loop fusion | bytes 96 | tf_op jit(solution)/shard_map/jit(dynamic_index_in_dim)/dynamic_slice | solution.py:17
  38.4 2.1 %copy.130 = bf16[12,8,8,512]{3,2,0,1:T(8,128)(2,1)} copy(bf16[12,8,8,512]{3,2,1,0:T(8,128)(2,1)} %bitcast.244) | data formatting | bytes 1572864 | tf_op jit(solution)/shard_map/all_to_all | solution.py:51
  40.5 1.6 %all-to-all-done.2 = bf16[96,8,256]{2,0,1:T(8,128)(2,1)S(1)} async-done(((bf16[96,8,256]{2,0,1:T(8,128)(2,1)}), bf16[96,8,256]{2,0,1:T(8,128)(2,1)S(1)}, u32[]{:S(2)}, u32[]{:S(2)}) %all-to-all-start.2) | async-done | bytes 393248 | tf_op jit(solution)/shard_map/all_to_all | solution.py:53
  42.1 6.1 %all-to-all-start.1 = ((bf16[96,8,512]{2,0,1:T(8,128)(2,1)}), bf16[96,8,512]{2,0,1:T(8,128)(2,1)S(1)}, u32[]{:S(2)}, u32[]{:S(2)}) async-start(bf16[96,8,512]{2,0,1:T(8,128)(2,1)} %bitcast.239), calls=%async_computation.1 | async-start | bytes 1572864 | tf_op jit(solution)/shard_map/all_to_all | solution.py:51
  49.4 2.4 %broadcast_compare_fusion = (pred[768,384]{0,1:T(8,128)(4,1)S(1)}, pred[768,384]{0,1:T(8,128)(4,1)}, pred[768,384]{0,1:T(8,128)(4,1)S(1)}, pred[768,384]{0,1:T(8...) fusion(s32[768]{0:T(1024)S(1)} %pad_add_fusion, ...), kind=kLoop, calls=%fused_computation.49 | loop fusion | flops 2359296 | bytes 2374656 | tf_op jit(solution)/shard_map/le | solution.py:28
  53.6 2.2 %collective-permute-start = (bf16[2,768,2,128]{3,1,2,0:T(8,128)(2,1)}, bf16[2,768,2,128]{3,1,2,0:T(8,128)(2,1)}, u32[]{:S(2)}, u32[]{:S(2)}) collective-permute-start(bf16[2,768,2,128]{3,1,2,0:T(8,128)(2,1)} %copy_dynamic-update-slice_fusion), channel_id=1, source_target_pairs={{0,1},{1,2},{2,3},{3,0},{4,5},{5,6},{6,7},{7,4},{8,9},{9,10},{10,1... | collective-permute-start | bytes 2359304 | tf_op jit(solution)/shard_map/while/body/eval_jaxpr/ppermute | solution.py:13
  56.5 10.7 %all-to-all-done.1 = bf16[96,8,512]{2,0,1:T(8,128)(2,1)S(1)} async-done(((bf16[96,8,512]{2,0,1:T(8,128)(2,1)}), bf16[96,8,512]{2,0,1:T(8,128)(2,1)S(1)}, u32[]{:S(2)}, u32[]{:S(2)}) %all-to-all-start.1) | async-done | bytes 786464 | tf_op jit(solution)/shard_map/all_to_all | solution.py:51
  67.4 2.8 %fusion = (f32[2,2,768]{2,1,0:T(2,128)S(1)}, f32[2,384,768,2]{2,1,3,0:T(8,128)S(1)}) fusion(pred[768,384]{0,1:T(8,128)(4,1)} %get-tuple-element.46, bf16[768,2,2,128]{3,2,1,0:T(2,128)(2,1)S(1)} %reshape.256, bf16[1,768,2,128]{3,1,2,0:T(8,128)(2,1)S(1)} %get-tuple-element.25), kind=kOutput, calls=%fused_computation.8 | convolution fusion | flops 306705408 | bytes 6008832 | tf_op jit(solution)/shard_map/rhgd,khd->hgrk/dot_general | solution.py:24
  70.2 1.8 %fusion.30 = f32[2,2,768,128]{2,3,1,0:T(8,128)S(1)} fusion(f32[2,384,768,2]{2,1,3,0:T(8,128)S(1)} %get-tuple-element.68, pred[768,384]{0,1:T(8,128)(4,1)S(1)} %copy-done.3, bf16[1,384,2,128]{1,3,2,0:T(8,128)(2,1)S(1)} %copy.89), kind=kOutput, calls=%fused_computation.31 | convolution fusion | flops 306708480 | bytes 6782976 | tf_op jit(solution)/shard_map/hgrk,khd->rhgd/dot_general | solution.py:31
  72.0 1.8 %fusion.2 = (f32[2,2,768]{2,1,0:T(2,128)S(1)}, f32[2,384,768,2]{2,1,3,0:T(8,128)S(1)}) fusion(pred[768,384]{0,1:T(8,128)(4,1)S(1)} %copy-done.2, bf16[768,2,2,128]{3,2,1,0:T(2,128)(2,1)S(1)} %reshape.256, bf16[1,768,2,128]{3,1,2,0:T(8,128)(2,1)S(1)} %get-tuple-element.25), kind=kOutput, calls=%fused_computation.10 | convolution fusion | flops 306705408 | bytes 6008832 | tf_op jit(solution)/shard_map/rhgd,khd->hgrk/dot_general | solution.py:24
  73.8 1.8 %fusion.28 = f32[2,2,768,128]{2,3,1,0:T(8,128)S(1)} fusion(f32[2,384,768,2]{2,1,3,0:T(8,128)S(1)} %get-tuple-element.70, pred[768,384]{0,1:T(8,128)(4,1)S(1)} %copy-done.2, bf16[1,384,2,128]{1,3,2,0:T(8,128)(2,1)S(1)} %copy.90), kind=kOutput, calls=%fused_computation.30 | convolution fusion | flops 306708480 | bytes 6782976 | tf_op jit(solution)/shard_map/hgrk,khd->rhgd/dot_general | solution.py:31
  75.6 3.5 %collective-permute-start.2 = (bf16[2,768,2,128]{3,1,2,0:T(8,128)(2,1)}, bf16[2,768,2,128]{3,1,2,0:T(8,128)(2,1)S(1)}, u32[]{:S(2)}, u32[]{:S(2)}) collective-permute-start(bf16[2,768,2,128]{3,1,2,0:T(8,128)(2,1)} %collective-permute-done), channel_id=1, source_target_pairs={{0,1},{1,2},{2,3},{3,0},{4,5},{5,6},{6,7},{7,4},{8,9},{9,10},{10,1... | collective-permute-start | bytes 2359304 | tf_op jit(solution)/shard_map/ppermute | solution.py:13
  79.1 2.7 %fusion.10 = (f32[2,2,768]{2,1,0:T(2,128)S(1)}, f32[2,384,768,2]{2,1,3,0:T(8,128)S(1)}) fusion(pred[768,384]{0,1:T(8,128)(4,1)S(1)} %copy-done.1, bf16[768,2,2,128]{3,2,1,0:T(2,128)(2,1)S(1)} %reshape.256, bf16[2,768,2,128]{3,1,2,0:T(8,128)(2,1)} %collective-permute-done.1), kind=kOutput, calls=%fused_computation.18 | convolution fusion | flops 306705408 | bytes 6008832 | tf_op jit(solution)/shard_map/while/body/eval_jaxpr/rhgd,khd->hgrk/dot_general | solution.py:24
  81.8 2.6 %fusion.20 = f32[2,128,2,768]{3,1,2,0:T(8,128)S(1)} fusion(f32[2,384,768,2]{2,1,3,0:T(8,128)S(1)} %get-tuple-element.60, pred[768,384]{0,1:T(8,128)(4,1)S(1)} %copy-done.1, bf16[2,768,2,128]{3,1,2,0:T(8,128)(2,1)} %collective-permute-done.1), kind=kOutput, calls=%fused_computation.26 | convolution fusion | flops 306708480 | bytes 6782976 | tf_op jit(solution)/shard_map/while/body/eval_jaxpr/hgrk,khd->rhgd/dot_general | solution.py:31
  84.4 2.7 %fusion.8 = (f32[2,2,768]{2,1,0:T(2,128)S(1)}, f32[2,384,768,2]{2,1,3,0:T(8,128)S(1)}) fusion(pred[768,384]{0,1:T(8,128)(4,1)S(1)} %copy-done, bf16[768,2,2,128]{3,2,1,0:T(2,128)(2,1)S(1)} %reshape.256, bf16[2,768,2,128]{3,1,2,0:T(8,128)(2,1)} %collective-permute-done.1), kind=kOutput, calls=%fused_computation.16 | convolution fusion | flops 306705408 | bytes 6008832 | tf_op jit(solution)/shard_map/while/body/eval_jaxpr/rhgd,khd->hgrk/dot_general | solution.py:24
  87.1 2.5 %fusion.22 = f32[2,128,2,768]{3,1,2,0:T(8,128)S(1)} fusion(f32[2,384,768,2]{2,1,3,0:T(8,128)S(1)} %get-tuple-element.62, pred[768,384]{0,1:T(8,128)(4,1)S(1)} %copy-done, bf16[2,768,2,128]{3,1,2,0:T(8,128)(2,1)} %collective-permute-done.1), kind=kOutput, calls=%fused_computation.27 | convolution fusion | flops 306708480 | bytes 6782976 | tf_op jit(solution)/shard_map/while/body/eval_jaxpr/hgrk,khd->rhgd/dot_general | solution.py:31
  89.7 2.7 %fusion.6 = (f32[2,2,768]{2,1,0:T(2,128)S(1)}, f32[2,384,768,2]{2,1,3,0:T(8,128)S(1)}) fusion(pred[768,384]{0,1:T(8,128)(4,1)S(1)} %get-tuple-element.40, bf16[768,2,2,128]{3,2,1,0:T(2,128)(2,1)S(1)} %reshape.256, bf16[2,768,2,128]{3,1,2,0:T(8,128)(2,1)} %collective-permute-done), kind=kOutput, calls=%fused_computation.14 | convolution fusion | flops 306705408 | bytes 6008832 | tf_op jit(solution)/shard_map/while/body/eval_jaxpr/rhgd,khd->hgrk/dot_general | solution.py:24
  92.4 2.5 %fusion.24 = f32[2,128,2,768]{3,1,2,0:T(8,128)S(1)} fusion(f32[2,384,768,2]{2,1,3,0:T(8,128)S(1)} %get-tuple-element.64, pred[768,384]{0,1:T(8,128)(4,1)S(1)} %get-tuple-element.40, bf16[2,768,2,128]{3,1,2,0:T(8,128)(2,1)} %collective-permute-done), kind=kOutput, calls=%fused_computation.28 | convolution fusion | flops 306708480 | bytes 6782976 | tf_op jit(solution)/shard_map/while/body/eval_jaxpr/hgrk,khd->rhgd/dot_general | solution.py:31
  94.9 2.7 %fusion.4 = (f32[2,2,768]{2,1,0:T(2,128)S(1)}, f32[2,384,768,2]{2,1,3,0:T(8,128)S(1)}) fusion(pred[768,384]{0,1:T(8,128)(4,1)S(1)} %get-tuple-element.29, bf16[768,2,2,128]{3,2,1,0:T(2,128)(2,1)S(1)} %reshape.256, bf16[2,768,2,128]{3,1,2,0:T(8,128)(2,1)} %collective-permute-done), kind=kOutput, calls=%fused_computation.12 | convolution fusion | flops 306705408 | bytes 6008832 | tf_op jit(solution)/shard_map/while/body/eval_jaxpr/rhgd,khd->hgrk/dot_general | solution.py:24
  97.6 2.7 %fusion.26 = f32[2,128,2,768]{3,1,2,0:T(8,128)S(1)} fusion(f32[2,384,768,2]{2,1,3,0:T(8,128)S(1)} %get-tuple-element.66, pred[768,384]{0,1:T(8,128)(4,1)S(1)} %get-tuple-element.29, bf16[2,768,2,128]{3,1,2,0:T(8,128)(2,1)} %collective-permute-done), kind=kOutput, calls=%fused_computation.29 | convolution fusion | flops 306708480 | bytes 6782976 | tf_op jit(solution)/shard_map/while/body/eval_jaxpr/hgrk,khd->rhgd/dot_general | solution.py:31
  100.4 1.8 %fusion.12 = (f32[2,2,768]{2,1,0:T(2,128)S(1)}, f32[2,384,768,2]{2,1,3,0:T(8,128)S(1)}) fusion(pred[768,384]{0,1:T(8,128)(4,1)S(1)} %get-tuple-element.45, bf16[768,2,2,128]{3,2,1,0:T(2,128)(2,1)S(1)} %reshape.256, bf16[2,768,2,128]{3,1,2,0:T(8,128)(2,1)S(1)} %collective-permute-done.2), kind=kOutput, calls=%fused_computation.20 | convolution fusion | flops 306705408 | bytes 6008832 | tf_op jit(solution)/shard_map/rhgd,khd->hgrk/dot_general | solution.py:24
  102.2 1.8 %fusion.14 = (f32[2,2,768]{2,1,0:T(2,128)S(1)}, f32[2,384,768,2]{2,1,3,0:T(8,128)S(1)}) fusion(pred[768,384]{0,1:T(8,128)(4,1)S(1)} %get-tuple-element.27, bf16[768,2,2,128]{3,2,1,0:T(2,128)(2,1)S(1)} %reshape.256, bf16[2,768,2,128]{3,1,2,0:T(8,128)(2,1)S(1)} %collective-permute-done.2), kind=kOutput, calls=%fused_computation.22 | convolution fusion | flops 306705408 | bytes 6008832 | tf_op jit(solution)/shard_map/rhgd,khd->hgrk/dot_general | solution.py:24
  104.0 1.6 %fusion.18 = f32[2,128,2,768]{3,1,2,0:T(8,128)S(1)} fusion(f32[2,384,768,2]{2,1,3,0:T(8,128)S(1)} %get-tuple-element.58, pred[768,384]{0,1:T(8,128)(4,1)S(1)} %get-tuple-element.45, bf16[2,768,2,128]{3,1,2,0:T(8,128)(2,1)S(1)} %collective-permute-done.2), kind=kOutput, calls=%fused_computation.25 | convolution fusion | flops 306708480 | bytes 6782976 | tf_op jit(solution)/shard_map/hgrk,khd->rhgd/dot_general | solution.py:31
  105.6 2.0 %fusion.41 = bf16[768,2,2,128]{0,3,2,1:T(8,128)(2,1)S(1)} fusion(f32[2,128,2,768]{3,1,2,0:T(8,128)S(1)} %fusion.18, f32[2,128,2,768]{3,1,2,0:T(8,128)S(1)} %fusion.20, f32[2,128,2,768]{3,1,2,0:T(8,128)S(1)} %fusion.22, f32[2,128,2,768]{3,1,2,0:T(8,128)S(1)} %fusion.24, f32[2,128,2,768]{3,1,2,0:T(8,128)S(1)} %fusion.26, f32[2,2,768,128]{2,3,1,0:T(8,128)S(1)} %fusion.30, ...), kind=kOutput, calls=%fused_computation.42 | convolution fusion | flops 310247424 | bytes 17018880 | tf_op jit(solution)/shard_map/hgrk,khd->rhgd/dot_general | solution.py:31
  (31 shorter events, 9.6 us)
Async XLA Ops:
  11.4 15.5 %all-to-all-start = ((bf16[8,96,256]{2,1,0:T(8,128)(2,1)}), bf16[8,96,256]{2,1,0:T(8,128)(2,1)S(1)}, u32[]{:S(2)}, u32[]{:S(2)}) async-start(bf16[8,96,256]{2,1,0:T(8,128)(2,1)} %bitcast_dynamic-update-slice_fusion), calls=%async_computation | async-start | bytes 786432 | tf_op jit(solution)/shard_map/all_to_all | solution.py:42
  26.9 15.2 %all-to-all-start.2 = ((bf16[96,8,256]{2,0,1:T(8,128)(2,1)}), bf16[96,8,256]{2,0,1:T(8,128)(2,1)S(1)}, u32[]{:S(2)}, u32[]{:S(2)}) async-start(bf16[96,8,256]{2,0,1:T(8,128)(2,1)} %bitcast.240), calls=%async_computation.2 | async-start | bytes 786432 | tf_op jit(solution)/shard_map/all_to_all | solution.py:53
  42.1 25.1 %all-to-all-start.1 = ((bf16[96,8,512]{2,0,1:T(8,128)(2,1)}), bf16[96,8,512]{2,0,1:T(8,128)(2,1)S(1)}, u32[]{:S(2)}, u32[]{:S(2)}) async-start(bf16[96,8,512]{2,0,1:T(8,128)(2,1)} %bitcast.239), calls=%async_computation.1 | async-start | bytes 1572864 | tf_op jit(solution)/shard_map/all_to_all | solution.py:51
  53.6 22.0 %collective-permute-start = (bf16[2,768,2,128]{3,1,2,0:T(8,128)(2,1)}, bf16[2,768,2,128]{3,1,2,0:T(8,128)(2,1)}, u32[]{:S(2)}, u32[]{:S(2)}) collective-permute-start(bf16[2,768,2,128]{3,1,2,0:T(8,128)(2,1)} %copy_dynamic-update-slice_fusion), channel_id=1, source_target_pairs={{0,1},{1,2},{2,3},{3,0},{4,5},{5,6},{6,7},{7,4},{8,9},{9,10},{10,1... | collective-permute-start | bytes 2359304 | tf_op jit(solution)/shard_map/while/body/eval_jaxpr/ppermute | solution.py:13
  55.9 23.2 %collective-permute-start.1 = (bf16[2,768,2,128]{3,1,2,0:T(8,128)(2,1)}, bf16[2,768,2,128]{3,1,2,0:T(8,128)(2,1)}, u32[]{:S(2)}, u32[]{:S(2)}) collective-permute-start(bf16[2,768,2,128]{3,1,2,0:T(8,128)(2,1)} %copy_dynamic-update-slice_fusion), channel_id=1, source_target_pairs={{0,3},{1,0},{2,1},{3,2},{4,7},{5,4},{6,5},{7,6},{8,11},{9,8},{10,9... | collective-permute-start | bytes 2359304 | tf_op jit(solution)/shard_map/while/body/eval_jaxpr/ppermute | solution.py:13
  67.4 2.8 %copy-start.3 = (pred[768,384]{0,1:T(8,128)(4,1)S(1)}, pred[768,384]{0,1:T(8,128)(4,1)}, u32[]{:S(2)}) copy-start(pred[768,384]{0,1:T(8,128)(4,1)} %get-tuple-element.46) | copy-start | bytes 884740
  70.2 1.8 %copy-start.2 = (pred[768,384]{0,1:T(8,128)(4,1)S(1)}, pred[768,384]{0,1:T(8,128)(4,1)}, u32[]{:S(2)}) copy-start(pred[768,384]{0,1:T(8,128)(4,1)} %get-tuple-element.28) | copy-start | bytes 884740
  73.8 5.3 %copy-start.1 = (pred[768,384]{0,1:T(8,128)(4,1)S(1)}, pred[768,384]{0,1:T(8,128)(4,1)}, u32[]{:S(2)}) copy-start(pred[768,384]{0,1:T(8,128)(4,1)} %get-tuple-element.44) | copy-start | bytes 884740
  75.6 24.8 %collective-permute-start.2 = (bf16[2,768,2,128]{3,1,2,0:T(8,128)(2,1)}, bf16[2,768,2,128]{3,1,2,0:T(8,128)(2,1)S(1)}, u32[]{:S(2)}, u32[]{:S(2)}) collective-permute-start(bf16[2,768,2,128]{3,1,2,0:T(8,128)(2,1)} %collective-permute-done), channel_id=1, source_target_pairs={{0,1},{1,2},{2,3},{3,0},{4,5},{5,6},{6,7},{7,4},{8,9},{9,10},{10,1... | collective-permute-start | bytes 2359304 | tf_op jit(solution)/shard_map/ppermute | solution.py:13
  81.8 2.6 %copy-start = (pred[768,384]{0,1:T(8,128)(4,1)S(1)}, pred[768,384]{0,1:T(8,128)(4,1)}, u32[]{:S(2)}) copy-start(pred[768,384]{0,1:T(8,128)(4,1)} %get-tuple-element.42) | copy-start | bytes 884740
